TPU v7x, 32 devices: a whole 2x2x4 slice. The times are simulated.
32 devices in a mesh: row: 4 (over y, x), col: 8 (over z, core).
Axes of the slice: x: 2, y: 2, z: 4, core: 2. Of those that a mesh axis runs over, the one named last changes fastest.
Arguments:
- activations: bfloat16 [1024, 9216], P('col', 'row'), may hold values from -64 to 64
- output_grads: bfloat16 [1024, 73728], P('row', 'col'), may hold values from -16 to 16
- weight: bfloat16 [9216, 73728], P('row', 'col'), may hold values from -1 to 1
- row_moment: float32 [9216], P('row'), may hold values from 0.01 to 0.3
- col_moment: float32 [73728], P('col'), may hold values from 0.01 to 0.3
Outputs:
- new_weight: bfloat16 [9216, 73728], P('row', 'col')
- new_row: float32 [9216], P('row')
- new_col: float32 [73728], P('col')
All inputs are finite; a program needn't handle non-finite values.
Results may differ from a plain program's by a relative error of at most 0.0004.
Values may be sent and summed in bfloat16 or wider, within the bound.
A program may use at most 256 MiB of HBM per device.

v0:
```python
import jax
import jax.numpy as jnp
from jax import lax
from jax.sharding import PartitionSpec as P

ADDED_SQUARE = 1e-30
DECAY_RATE = 0.8
CLIP_LIMIT = 1.0
STEP_SIZE = 0.1
MEAN_OFFSET = 1e-06


def on_device(activations, output_grads, weight, row_moment, col_moment):
    tile_rows, tile_cols = weight.shape
    total_rows = tile_rows * lax.axis_size("row")
    total_cols = tile_cols * lax.axis_size("col")
    entries = float(total_rows * total_cols)
    weight_wide = weight.astype(jnp.float32)
    weight_local = jnp.sum(weight_wide * weight_wide)
    weight_total = lax.psum(weight_local, ("row", "col"))
    contract = (((0,), (0,)), ((), ()))
    acts_all = lax.all_gather(activations, "col", axis=0, tiled=True)
    gradient = lax.dot_general(
        acts_all,
        lax.all_gather(output_grads, "row", axis=0, tiled=True),
        contract,
        preferred_element_type=jnp.float32,
    )
    squared = gradient * gradient
    row_part = jnp.sum(squared + ADDED_SQUARE, axis=1)
    col_part = jnp.sum(squared + ADDED_SQUARE, axis=0)
    row_total = lax.psum(row_part, "col")
    col_total = lax.psum(col_part, "row")
    new_row = DECAY_RATE * row_moment + (1.0 - DECAY_RATE) * row_total / total_cols
    new_col = DECAY_RATE * col_moment + (1.0 - DECAY_RATE) * col_total / total_rows
    inverse = lax.rsqrt(new_row[:, None] * new_col[None, :])
    ratio_local = jnp.sum(squared * inverse * inverse)
    leader = (lax.axis_index("col") == 0).astype(jnp.float32)
    row_local = leader * jnp.sum(new_row)
    row_sum, ratio_sum = lax.psum((row_local, ratio_local), ("row", "col"))
    row_mean = row_sum / total_rows
    rms_update = jnp.sqrt(row_mean * ratio_sum / entries)
    clip_factor = jnp.maximum(1.0, rms_update / CLIP_LIMIT)
    step_scale = STEP_SIZE * jnp.sqrt(weight_total / entries + MEAN_OFFSET)
    update = gradient * inverse * jnp.sqrt(row_mean)
    new_weight = (weight_wide - step_scale / clip_factor * update).astype(jnp.bfloat16)
    return (new_weight, new_row, new_col)


def solution(mesh):
    return jax.shard_map(
        on_device,
        mesh=mesh,
        in_specs=(P("col", "row"), P("row", "col"), P("row", "col"), P("row"), P("col")),
        out_specs=(P("row", "col"), P("row"), P("col")),
        check_vma=False,
    )
```

profile of v0, /device:TPU:0, one launch (start us, length us, event | category | flops | bytes accessed | tf_op | source)
XLA Modules:
  0.0 470.4 jit_solution(5277439258976595096)
XLA Ops:
  7.2 0.0 all-gather.3.cloned.1.call-start
  7.2 0.7 all-gather.3.cloned.1.call-update
  7.9 0.0 all-gather.5.cloned.1.call-start
  7.9 0.7 all-gather.5.cloned.1.call-update
  8.7 24.5 %fusion = f32[]{:T(128)} fusion(bf16[2304,9216]{1,0:T(8,128)(2,1)} %param.7), kind=kLoop, calls=%fused_computation.3 | loop fusion | flops 63700992 | bytes 42467332 | tf_op jit(solution)/shard_map/reduce_sum | solution.py:19
  33.1 0.0 copy-start.2
  33.2 0.0 copy-start.3
  33.2 30.4 %all-gather.3.cloned.1.call-done = bf16[1024,2304]{1,0:T(8,128)(2,1)} async-done(((bf16[128,2304]{1,0:T(8,128)(2,1)}), bf16[1024,2304]{1,0:T(8,128)(2,1)}) %all-gather.3.cloned.1.call-update) | async-done | bytes 4718608 | tf_op jit(solution)/shard_map/all_gather | solution.py:22
  63.6 176.5 %all-gather.5.cloned.1.call-done = bf16[1024,9216]{1,0:T(8,128)(2,1)} async-done(((bf16[256,9216]{1,0:T(8,128)(2,1)}), bf16[1024,9216]{1,0:T(8,128)(2,1)}) %all-gather.5.cloned.1.call-update) | async-done | bytes 18874384 | tf_op jit(solution)/shard_map/all_gather | solution.py:25
  240.0 59.5 %add_reduce_fusion = (f32[9216]{0:T(1024)S(1)}, f32[2304]{0:T(1024)S(1)}, f32[2304,9216]{1,0:T(8,128)}) fusion(bf16[1024,2304]{1,0:T(8,128)(2,1)} %all-gather.3.cloned.1.call-done, bf16[1024,9216]{1,0:T(8,128)(2,1)} %all-gather.5.cloned.1.call-done), kind=kOutput, calls=%fused_computation.7 | convolution fusion | flops 43571466240 | bytes 108573696 | tf_op jit(solution)/shard_map/dot_general | solution.py:23
  299.5 15.8 %psum.38 = f32[9216]{0:T(1024)S(1)} all-reduce(f32[9216]{0:T(1024)S(1)} %get-tuple-element.3), channel_id=1, replica_groups=mesh['row'=4,'col'=8] {'row'}, use_global_device_ids=true, to_apply=%region_7.0 | all-reduce | flops 9216 | bytes 73728 | tf_op jit(solution)/shard_map/psum | solution.py:33
  315.4 25.9 %psum.36 = f32[2304]{0:T(1024)S(1)} all-reduce(f32[2304]{0:T(1024)S(1)} %get-tuple-element.4), channel_id=1, replica_groups=mesh['row'=4,'col'=8] {'col'}, use_global_device_ids=true, to_apply=%region_3.0 | all-reduce | flops 2304 | bytes 18432 | tf_op jit(solution)/shard_map/psum | solution.py:32
  341.3 0.0 copy-done.2
  341.3 0.0 copy-done.3
  341.3 0.0 copy-start
  341.3 0.6 fusion.3
  341.9 0.0 copy-start.1
  341.9 28.1 %fusion.2 = f32[]{:T(128)} fusion(f32[2304,9216]{1,0:T(8,128)} %get-tuple-element.10, f32[9216]{0:T(1024)S(1)} %multiply_add_fusion, f32[2304]{0:T(1024)S(1)} %get-tuple-element.9), kind=kLoop, calls=%fused_computation.5 | loop fusion | flops 106168320 | bytes 84980736 | tf_op jit(solution)/shard_map/reduce_sum | solution.py:37
  370.6 37.2 %all-reduce = (f32[]{:T(128)}, f32[]{:T(128)}, f32[]{:T(128)}) all-reduce(f32[]{:T(128)S(6)} %mul.66, f32[]{:T(128)} %fusion, f32[]{:T(128)} %fusion.2), channel_id=1, replica_groups=mesh['row'=4,'col'=8] {'row','col'}, use_global_device_ids=true, to_apply=%region_5.0 | all-reduce | flops 3 | bytes 24 | tf_op jit(solution)/shard_map/psum | solution.py:40
  409.8 53.7 %fusion.1 = bf16[2304,9216]{1,0:T(8,128)(2,1)} fusion(bf16[2304,9216]{1,0:T(8,128)(2,1)} %param.7, f32[2304,9216]{1,0:T(8,128)} %get-tuple-element.10, f32[]{:T(128)S(6)} %sqrt.11, f32[]{:T(128)S(6)} %div.32, f32[9216]{0:T(1024)S(1)} %multiply_add_fusion, f32[2304]{0:T(1024)S(1)} %get-tuple-element.9), kind=kLoop, calls=%fused_computation.4 | loop fusion | flops 148635648 | bytes 169915392 | tf_op jit(solution)/shard_map/convert_element_type | solution.py:46
  463.5 0.0 copy-done
  463.5 0.0 copy-done.1
  (1 shorter events, 0.0 us)
Async XLA Ops:
  7.2 56.4 %all-gather.3.cloned.1.call-start = ((), (), s32[]{:S(2)}) async-start(), calls=%async_computation | async-start | bytes 5308416 | tf_op jit(solution)/shard_map/all_gather | solution.py:22
  7.9 232.1 %all-gather.5.cloned.1.call-start = ((), (), s32[]{:S(2)}) async-start(), calls=%async_computation.1 | async-start | bytes 23592960 | tf_op jit(solution)/shard_map/all_gather | solution.py:25
  33.1 308.1 %copy-start.2 = (f32[9216]{0:T(1024)S(1)}, f32[9216]{0:T(1024)}, u32[]{:S(2)}) copy-start(f32[9216]{0:T(1024)} %param.9) | copy-start | bytes 110596
  33.2 308.1 %copy-start.3 = (f32[2304]{0:T(1024)S(1)}, f32[2304]{0:T(1024)}, u32[]{:S(2)}) copy-start(f32[2304]{0:T(1024)} %param.8) | copy-start | bytes 27652
  341.3 122.2 %copy-start = (f32[9216]{0:T(1024)}, f32[9216]{0:T(1024)S(1)}, u32[]{:S(2)}) copy-start(f32[9216]{0:T(1024)S(1)} %multiply_add_fusion) | copy-start | bytes 110596
  341.9 121.6 %copy-start.1 = (f32[2304]{0:T(1024)}, f32[2304]{0:T(1024)S(1)}, u32[]{:S(2)}) copy-start(f32[2304]{0:T(1024)S(1)} %get-tuple-element.9) | copy-start | bytes 27652
Sparse Core Ops, SparseCore 0:
  9.6 53.9 all-gather.2
  65.4 174.5 all-gather.4
where the time goes:
time: 472 us; the launch traced here: 470 us
  waiting for transfers between devices  208 us (44%)
  other arithmetic  107 us (23%)
  blocking collectives  78.9 us (17%)
  matrix products  59.5 us (13%)
  between operations  16.8 us (4%)
    all_gather x1, waiting for transfers between devices, on_device(): lax.all_gather(output_grads, 'row', axis=0, tiled=True)  176 us
    dot_general x1, matrix products, on_device(): lax.dot_general(acts_all, lax.all_gather(output_grads, 'row', axis=0, til...  59.5 us
    convert_element_type x1, other arithmetic, on_device(): (weight_wide - step_scale / clip_factor * update).astype(jnp.bfloat16)  53.7 us
    psum x1, blocking collectives, on_device(): row_sum, ratio_sum = lax.psum((row_local, ratio_local), ('row', 'col'))  37.2 us
    all_gather x1, waiting for transfers between devices, on_device(): acts_all = lax.all_gather(activations, 'col', axis=0, tiled=True)  30.4 us
    reduce_sum x1, other arithmetic, on_device(): ratio_local = jnp.sum(squared * inverse * inverse)  28.1 us
    psum x1, blocking collectives, on_device(): row_total = lax.psum(row_part, 'col')  25.9 us
    reduce_sum x1, other arithmetic, on_device(): weight_local = jnp.sum(weight_wide * weight_wide)  24.5 us
  transfers between devices with their start and end apart: 2, of which 2 were waited for; matrix products, arithmetic and copies ran while one was open for 5% of the time, Pallas kernels for 0%

commit v1 on v0

--- a/solution.py
+++ b/solution.py
@@ -1,6 +1,10 @@
+import functools
+
 import jax
 import jax.numpy as jnp
 from jax import lax
+from jax.experimental import pallas as pl
+from jax.experimental.pallas import tpu as pltpu
 from jax.sharding import PartitionSpec as P
 
 ADDED_SQUARE = 1e-30
@@ -9,8 +13,422 @@
 STEP_SIZE = 0.1
 MEAN_OFFSET = 1e-06
 
-
-def on_device(activations, output_grads, weight, row_moment, col_moment):
+MESH = pl.DeviceIdType.MESH
+WIDTH = 512
+TALL = 768
+KEPT = 192
+SUB = 256
+AHEAD = 2
+LAG = 2
+SLOTS = LAG + 1
+ACTS_FORWARD = 3
+ACTS_READY = 5
+
+
+def lane_sum(x):
+    out = x[:, :128]
+    for k in range(1, x.shape[1] // 128):
+        out = out + x[:, k * 128 : (k + 1) * 128]
+    return out
+
+
+def sublane_sum(x):
+    return jnp.sum(x.reshape(x.shape[0] // 8, 8, x.shape[1]), axis=0)
+
+
+def gather_kernel(
+    rows, cols,
+    acts_ref, og_ref, w_ref, rm_ref, cm_ref,
+    og_out, at_out, g_out, nr_out, nc_out, rs_out, cs_out,
+    og_all, acts_all, acts_t, grad, wbuf, rowacc, sacc, wacc, colx, rowx, scb, scc,
+    load_sem, og_sem, acts_sem, sib_sem, col_sem, row_sem, scb_sem, scc_sem, w_sem, out_sem, g_sem, misc_sem,
+):
+    n, tokens, width = og_all.shape
+    tile_rows = acts_t.shape[0]
+    blocks = tile_rows // TALL
+    share = tokens // rows
+    half = share // 2
+    wrows = tile_rows // n
+    total_rows = tile_rows * rows
+    total_cols = n * width * cols
+    entries = float(total_rows * total_cols)
+    r, c = lax.axis_index("row"), lax.axis_index("col")
+    rx = r + 1 - 2 * lax.rem(r, 2)
+    ry = lax.rem(r + 2, 4)
+    rd = lax.rem(rx + 2, 4)
+    sib = c + 1 - 2 * lax.rem(c, 2)
+
+    def region(owner, start, size):
+        return pl.ds(pl.multiple_of(owner * share + start, half), size)
+
+    def load(j):
+        return pltpu.make_async_copy(
+            og_ref.at[:, pl.ds(pl.multiple_of(j * width, width), width)],
+            og_all.at[j, region(r, 0, share), :], load_sem.at[j])
+
+    def og_copy(j, kind, owner, start, size, to):
+        ref = og_all.at[j, region(owner, start, size), :]
+        return pltpu.make_async_remote_copy(
+            src_ref=ref, dst_ref=ref, send_sem=og_sem.at[0, kind, j], recv_sem=og_sem.at[1, kind, j],
+            device_id={"row": to}, device_id_type=MESH)
+
+    def own_x(j):
+        return og_copy(j, 0, r, 0, share, rx)
+
+    def own_y(j):
+        return og_copy(j, 1, r, 0, share, ry)
+
+    def fwd_y(j):
+        return og_copy(j, 2, rx, 0, half, ry)
+
+    def fwd_x(j):
+        return og_copy(j, 3, ry, half, half, rx)
+
+    def acts_copy(d):
+        to = lax.rem(c + 2 * d, cols)
+        return pltpu.make_async_remote_copy(
+            src_ref=acts_all.at[c], dst_ref=acts_all.at[c], send_sem=acts_sem.at[0, d], recv_sem=acts_sem.at[1, d],
+            device_id={"col": to}, device_id_type=MESH)
+
+    def sib_copy(d):
+        at = lax.rem(c + cols - 2 * d, cols)
+        return pltpu.make_async_remote_copy(
+            src_ref=acts_all.at[at], dst_ref=acts_all.at[at], send_sem=sib_sem.at[0, d], recv_sem=sib_sem.at[1, d],
+            device_id={"col": sib}, device_id_type=MESH)
+
+    def col_copy(j, d):
+        return pltpu.make_async_remote_copy(
+            src_ref=colx.at[r, j], dst_ref=colx.at[r, j], send_sem=col_sem.at[0, d, j], recv_sem=col_sem.at[1, d, j],
+            device_id={"row": lax.rem(r + d, rows)}, device_id_type=MESH)
+
+    def row_copy(d):
+        return pltpu.make_async_remote_copy(
+            src_ref=rowx.at[c], dst_ref=rowx.at[c], send_sem=row_sem.at[0, d], recv_sem=row_sem.at[1, d],
+            device_id={"col": lax.rem(c + d, cols)}, device_id_type=MESH)
+
+    def scb_copy(d):
+        return pltpu.make_async_remote_copy(
+            src_ref=scb.at[c], dst_ref=scb.at[c], send_sem=scb_sem.at[0, d], recv_sem=scb_sem.at[1, d],
+            device_id={"col": lax.rem(c + d, cols)}, device_id_type=MESH)
+
+    def scc_copy(d):
+        return pltpu.make_async_remote_copy(
+            src_ref=scc.at[r], dst_ref=scc.at[r], send_sem=scc_sem.at[0, d], recv_sem=scc_sem.at[1, d],
+            device_id={"row": lax.rem(r + d, rows)}, device_id_type=MESH)
+
+    def w_copy(j):
+        return pltpu.make_async_copy(
+            w_ref.at[pl.ds(pl.multiple_of(j * wrows, wrows), wrows), :], wbuf.at[lax.rem(j, 2)], w_sem.at[lax.rem(j, 2)])
+
+    def og_store(j):
+        return pltpu.make_async_copy(og_all.at[j], og_out.at[j], out_sem.at[j])
+
+    def g_store(j):
+        s = lax.rem(j, SLOTS)
+        return pltpu.make_async_copy(grad.at[s, :, pl.ds(TALL - KEPT, KEPT), :], g_out.at[j], g_sem.at[s])
+
+    acts_load = pltpu.make_async_copy(acts_ref, acts_all.at[c], misc_sem.at[0])
+    acts_store = pltpu.make_async_copy(acts_t, at_out, misc_sem.at[1])
+
+    acts_load.start()
+
+    @pl.loop(0, n)
+    def _(j):
+        load(j).start()
+
+    w_copy(0).start()
+    w_copy(1).start()
+
+    barrier = pltpu.get_barrier_semaphore()
+    for d in range(1, rows):
+        pl.semaphore_signal(barrier, inc=1, device_id={"row": lax.rem(r + d, rows)}, device_id_type=MESH)
+    for d in range(1, cols):
+        pl.semaphore_signal(barrier, inc=1, device_id={"col": lax.rem(c + d, cols)}, device_id_type=MESH)
+    rowacc[...] = jnp.zeros_like(rowacc)
+    sacc[...] = jnp.zeros_like(sacc)
+    wacc[...] = jnp.zeros_like(wacc)
+    pl.semaphore_wait(barrier, rows + cols - 2)
+
+    def send_own(j):
+        load(j).wait()
+        own_x(j).start()
+        own_y(j).start()
+
+    for j in range(AHEAD):
+        send_own(j)
+    acts_load.wait()
+    for d in range(1, cols // 2):
+        acts_copy(d).start()
+    sib_copy(0).start()
+
+    def exchange(j):
+        own_x(j).wait_recv()
+        fwd_y(j).start()
+        own_y(j).wait_recv()
+        fwd_x(j).start()
+
+        @pl.when(j + AHEAD < n)
+        def _():
+            send_own(j + AHEAD)
+
+    def weigh(j):
+        w_copy(j).wait()
+        s = lax.rem(j, 2)
+        wide = 1024
+
+        @pl.loop(0, wbuf.shape[2] // wide)
+        def _(k):
+            x = wbuf[s, :, pl.ds(pl.multiple_of(k * wide, wide), wide)].astype(jnp.float32)
+            wacc[...] += sublane_sum(x * x)
+
+        @pl.when(j + 2 < n)
+        def _():
+            w_copy(j + 2).start()
+
+    def stats(k):
+        for d in range(1, rows):
+            col_copy(k, d).wait_recv()
+        total = colx[0, k]
+        for q in range(1, rows):
+            total = total + colx[q, k]
+        factor = DECAY_RATE * cm_ref[k] + (1.0 - DECAY_RATE) * total / total_rows
+        nc_out[k] = factor
+        cs_out[k] = lax.rsqrt(factor)
+        weight = 1.0 / factor
+        s = lax.rem(k, SLOTS)
+        for b in range(blocks):
+            @pl.loop(0, TALL // SUB)
+            def _(i):
+                at = pl.ds(pl.multiple_of(i * SUB, SUB), SUB)
+                g = grad[s, b, at, :]
+                to = pl.ds(pl.multiple_of(b * TALL + i * SUB, SUB), SUB)
+                sacc[to, :] += lane_sum(g * g * weight)
+
+    def compute(k):
+        fwd_y(k).wait_recv()
+        fwd_x(k).wait_recv()
+        og_store(k).start()
+        s = lax.rem(k, SLOTS)
+
+        @pl.when(k >= SLOTS)
+        def _():
+            g_store(k - SLOTS).wait()
+
+        right = og_all.at[k]
+        column = jnp.zeros((8, width), jnp.float32)
+        for b in range(blocks):
+            def step(i, column):
+                to = pl.ds(pl.multiple_of(b * TALL + i * SUB, SUB), SUB)
+                g = jnp.dot(acts_t[to, :], right[...], preferred_element_type=jnp.float32)
+                grad[s, b, pl.ds(pl.multiple_of(i * SUB, SUB), SUB), :] = g
+                squared = g * g + ADDED_SQUARE
+                rowacc[to, :] += lane_sum(squared)
+                return column + sublane_sum(squared)
+            column = lax.fori_loop(0, TALL // SUB, step, column)
+        colx[r, k] = jnp.sum(column, axis=0, keepdims=True)
+        for d in range(1, rows):
+            col_copy(k, d).start()
+        g_store(k).start()
+
+        @pl.when(k >= LAG)
+        def _():
+            stats(k - LAG)
+
+    def reach(j):
+        return jnp.minimum(j, 2 * (j - ACTS_READY + 1))
+
+    @pl.loop(0, ACTS_FORWARD)
+    def _(j):
+        exchange(j)
+        weigh(j)
+
+    for d in range(1, cols // 2):
+        acts_copy(d).wait_recv()
+        sib_copy(d).start()
+
+    @pl.loop(ACTS_FORWARD, ACTS_READY)
+    def _(j):
+        exchange(j)
+        weigh(j)
+
+    for d in range(cols // 2):
+        sib_copy(d).wait_recv()
+    part = acts_all.shape[1]
+    for q in range(cols):
+        acts_t[:, q * part : (q + 1) * part] = acts_all[q].T
+    acts_store.start()
+
+    @pl.loop(ACTS_READY, n)
+    def _(j):
+        exchange(j)
+        weigh(j)
+
+        @pl.loop(reach(j - 1), reach(j))
+        def _(k):
+            compute(k)
+
+    @pl.loop(n - 1, n)
+    def _(k):
+        compute(k)
+
+    rowx[c] = jnp.sum(rowacc[...].T, axis=0, keepdims=True)
+    for d in range(1, cols):
+        row_copy(d).start()
+
+    @pl.loop(n - LAG, n)
+    def _(k):
+        stats(k)
+
+    ratio_rows = jnp.sum(sacc[...].T, axis=0, keepdims=True)
+    for d in range(1, cols):
+        row_copy(d).wait_recv()
+    row_total = rowx[0]
+    for q in range(1, cols):
+        row_total = row_total + rowx[q]
+    new_row = DECAY_RATE * rm_ref[...] + (1.0 - DECAY_RATE) * row_total / total_cols
+    nr_out[...] = new_row
+
+    def spread(x):
+        return jnp.broadcast_to(jnp.sum(x, axis=1, keepdims=True), (1, 128))
+
+    scb[c, 0:1, :] = spread(ratio_rows / new_row)
+    scb[c, 1:2, :] = spread(jnp.sum(wacc[...], axis=0, keepdims=True))
+    for d in range(1, cols):
+        scb_copy(d).start()
+    row_sum = spread(new_row)
+    for d in range(1, cols):
+        scb_copy(d).wait_recv()
+    both = scb[0]
+    for q in range(1, cols):
+        both = both + scb[q]
+    scc[r, 0:2, :] = both[0:2, :]
+    scc[r, 2:3, :] = row_sum
+    for d in range(1, rows):
+        scc_copy(d).start()
+    root = lax.rsqrt(new_row)
+    for d in range(1, rows):
+        scc_copy(d).wait_recv()
+    every = scc[0]
+    for q in range(1, rows):
+        every = every + scc[q]
+    row_mean = every[2:3, :] / total_rows
+    rms_update = jnp.sqrt(row_mean * (every[0:1, :] / entries))
+    clip_factor = jnp.maximum(1.0, rms_update / CLIP_LIMIT)
+    step_scale = STEP_SIZE * jnp.sqrt(every[1:2, :] / entries + MEAN_OFFSET)
+    scale = step_scale / clip_factor * jnp.sqrt(row_mean)
+    rs_out[...] = jnp.broadcast_to(root, (128, tile_rows)).T * scale
+
+    @pl.loop(0, n)
+    def _(j):
+        own_x(j).wait_send()
+        own_y(j).wait_send()
+        fwd_y(j).wait_send()
+        fwd_x(j).wait_send()
+        og_store(j).wait()
+        for d in range(1, rows):
+            col_copy(j, d).wait_send()
+
+    @pl.loop(n - SLOTS, n)
+    def _(j):
+        g_store(j).wait()
+
+    acts_store.wait()
+    for d in range(1, cols // 2):
+        acts_copy(d).wait_send()
+    for d in range(cols // 2):
+        sib_copy(d).wait_send()
+    for d in range(1, cols):
+        row_copy(d).wait_send()
+        scb_copy(d).wait_send()
+    for d in range(1, rows):
+        scc_copy(d).wait_send()
+
+
+def update_kernel(at_ref, og_ref, w_ref, g_ref, rs_ref, cs_ref, out_ref):
+    i = pl.program_id(1)
+    tall, width = w_ref.shape
+    cs = cs_ref[0]
+    sub = KEPT
+
+    def finish(g, at):
+        rs = rs_ref[at, :]
+        wide = jnp.concatenate([rs] * (width // 128), axis=1)
+        out_ref[at, :] = (w_ref[at, :].astype(jnp.float32) - g * wide * cs).astype(out_ref.dtype)
+
+    finish(g_ref[0, 0], pl.ds(tall - KEPT, KEPT))
+    for k in range((tall - KEPT) // sub):
+        left = at_ref[pl.ds(pl.multiple_of(i * tall + k * sub, sub), sub), :]
+        g = jnp.dot(left, og_ref[0], preferred_element_type=jnp.float32)
+        finish(g, pl.ds(k * sub, sub))
+
+
+def with_kernels(rows, cols, activations, output_grads, weight, row_moment, col_moment):
+    tile_rows, tile_cols = weight.shape
+    part = activations.shape[0]
+    tokens = part * cols
+    n, width = tile_cols // WIDTH, WIDTH
+    blocks = tile_rows // TALL
+    f32, bf16 = jnp.float32, jnp.bfloat16
+    any_space = pl.BlockSpec(memory_space=pl.ANY)
+    vmem = pl.BlockSpec(memory_space=pltpu.VMEM)
+    dma = pltpu.SemaphoreType.DMA
+    flops = 2 * tile_rows * tile_cols * tokens
+    og_all, acts_t, kept, new_row, new_col, rs, cs = pl.pallas_call(
+        functools.partial(gather_kernel, rows, cols),
+        out_shape=(
+            jax.ShapeDtypeStruct((n, tokens, width), bf16),
+            jax.ShapeDtypeStruct((tile_rows, tokens), bf16),
+            jax.ShapeDtypeStruct((n, blocks, KEPT, width), f32),
+            jax.ShapeDtypeStruct((1, tile_rows), f32),
+            jax.ShapeDtypeStruct((n, 1, width), f32),
+            jax.ShapeDtypeStruct((tile_rows, 128), f32),
+            jax.ShapeDtypeStruct((n, 1, width), f32),
+        ),
+        in_specs=[any_space, any_space, any_space, vmem, vmem],
+        out_specs=(any_space, any_space, any_space, vmem, vmem, vmem, vmem),
+        scratch_shapes=[
+            pltpu.VMEM((n, tokens, width), bf16),
+            pltpu.VMEM((cols, part, tile_rows), bf16),
+            pltpu.VMEM((tile_rows, tokens), bf16),
+            pltpu.VMEM((SLOTS, blocks, TALL, width), f32),
+            pltpu.VMEM((2, tile_rows // n, tile_cols), bf16),
+            pltpu.VMEM((tile_rows, 128), f32),
+            pltpu.VMEM((tile_rows, 128), f32),
+            pltpu.VMEM((8, 1024), f32),
+            pltpu.VMEM((rows, n, 1, width), f32),
+            pltpu.VMEM((cols, 1, tile_rows), f32),
+            pltpu.VMEM((cols, 2, 128), f32),
+            pltpu.VMEM((rows, 3, 128), f32),
+            dma((n,)), dma((2, 4, n)), dma((2, cols // 2)), dma((2, cols // 2)), dma((2, rows, n)),
+            dma((2, cols)), dma((2, cols)), dma((2, rows)), dma((2,)), dma((n,)), dma((SLOTS,)), dma((2,)),
+        ],
+        compiler_params=pltpu.CompilerParams(
+            collective_id=0, has_side_effects=True, vmem_limit_bytes=62 * 1024 * 1024),
+        cost_estimate=pl.CostEstimate(flops=flops, bytes_accessed=2 * weight.size, transcendentals=0),
+        name="gather_stats",
+    )(activations, output_grads, weight, row_moment.reshape(1, tile_rows), col_moment.reshape(n, 1, width))
+    new_weight = pl.pallas_call(
+        update_kernel,
+        grid=(n, blocks),
+        out_shape=jax.ShapeDtypeStruct((tile_rows, tile_cols), bf16),
+        in_specs=[
+            pl.BlockSpec((tile_rows, tokens), lambda j, i: (0, 0)),
+            pl.BlockSpec((1, tokens, width), lambda j, i: (j, 0, 0)),
+            pl.BlockSpec((TALL, width), lambda j, i: (i, j)),
+            pl.BlockSpec((1, 1, KEPT, width), lambda j, i: (j, i, 0, 0)),
+            pl.BlockSpec((TALL, 128), lambda j, i: (i, 0)),
+            pl.BlockSpec((1, 1, width), lambda j, i: (j, 0, 0)),
+        ],
+        out_specs=pl.BlockSpec((TALL, width), lambda j, i: (i, j)),
+        compiler_params=pltpu.CompilerParams(
+            dimension_semantics=("arbitrary", "arbitrary"), vmem_limit_bytes=48 * 1024 * 1024),
+        cost_estimate=pl.CostEstimate(flops=flops, bytes_accessed=4 * weight.size, transcendentals=0),
+        name="update_weight",
+    )(acts_t, og_all, weight, kept, rs, cs)
+    return new_weight, new_row.reshape(tile_rows), new_col.reshape(tile_cols)
+
+
+def plain(activations, output_grads, weight, row_moment, col_moment):
     tile_rows, tile_cols = weight.shape
     total_rows = tile_rows * lax.axis_size("row")
     total_cols = tile_cols * lax.axis_size("col")
@@ -47,9 +465,22 @@
     return (new_weight, new_row, new_col)
 
 
+def on_device(rows, cols, activations, output_grads, weight, row_moment, col_moment):
+    tile_rows, tile_cols = weight.shape
+    chunks = tile_cols // WIDTH
+    fits = (
+        rows == 4 and cols % 2 == 0 and cols > 2
+        and tile_rows % TALL == 0 and tile_cols % 1024 == 0
+        and chunks > ACTS_READY + SLOTS and tile_rows % (16 * chunks) == 0
+        and output_grads.shape[0] % 32 == 0 and activations.shape[0] % 128 == 0
+    )
+    args = (activations, output_grads, weight, row_moment, col_moment)
+    return with_kernels(rows, cols, *args) if fits else plain(*args)
+
+
 def solution(mesh):
     return jax.shard_map(
-        on_device,
+        functools.partial(on_device, mesh.shape["row"], mesh.shape["col"]),
         mesh=mesh,
         in_specs=(P("col", "row"), P("row", "col"), P("row", "col"), P("row"), P("col")),
         out_specs=(P("row", "col"), P("row"), P("col")),

time: 472 us -> 282 us (0.60)
  Pallas kernels: 0 us -> 273 us
  waiting for transfers between devices: 208 us -> 0 us
  other arithmetic: 107 us -> 0.63 us
  blocking collectives: 78.9 us -> 0 us
  matrix products: 59.5 us -> 0 us
  between operations: 16.8 us -> 0.65 us
  local copies, waits for them, and re-layouts: 0.02 us -> 6.31 us
    pallas_call x0 -> x2, Pallas kernels: none -> 273 us  [the longest x1 200 us: with_kernels(): pl.pallas_call(functools.partial(gather_kernel, rows, cols), out_shape=(j...]
    all_gather x2 -> x0, waiting for transfers between devices: 207 us -> none  [the longest x1 176 us: on_device(): lax.all_gather(output_grads, 'row', axis=0, tiled=True)]
    psum x3 -> x0, blocking collectives: 78.9 us -> none  [the longest x1 37.2 us: on_device(): row_sum, ratio_sum = lax.psum((row_local, ratio_local), ('row', 'col'))]
    dot_general x1 -> x0, matrix products: 59.5 us -> none  [on_device(): lax.dot_general(acts_all, lax.all_gather(output_grads, 'row', axis=0, til...]
    convert_element_type x1 -> x0, other arithmetic: 53.7 us -> none  [on_device(): (weight_wide - step_scale / clip_factor * update).astype(jnp.bfloat16)]
    reduce_sum x3 -> x0, other arithmetic: 53.2 us -> none  [the longest x1 28.1 us: on_device(): ratio_local = jnp.sum(squared * inverse * inverse)]
    unnamed x8 -> x11, local copies, waits for them, and re-layouts: 0.02 us -> 4.99 us
  transfers between devices with their start and end apart: 2 -> 0, of which waited for: 2 -> 0; matrix products, arithmetic and copies ran while one was open for 5% -> 0% of each run, Pallas kernels for 0% -> 0%
where the time goes in v1:
time: 282 us; the launch traced here: 280 us
  Pallas kernels  273 us (97%)
  local copies, waits for them, and re-layouts  6.31 us (2%)
    pallas_call x1, Pallas kernels, with_kernels(): pl.pallas_call(functools.partial(gather_kernel, rows, cols), out_shape=(j...  200 us
    pallas_call x1, Pallas kernels, with_kernels(): pl.pallas_call(update_kernel, grid=(n, blocks), out_shape=jax.ShapeDtypeS...  72.9 us

profile of v1, /device:TPU:0, one launch (start us, length us, event | category | flops | bytes accessed | tf_op | source)
XLA Modules:
  0.0 280.5 jit_solution(15595642800194720436)
XLA Ops:
  0.6 1.3 reshape.18.rm_ref
  1.9 199.9 %gather_stats.1 = (bf16[18,1024,512]{2,1,0:T(8,128)(2,1)}, bf16[2304,1024]{1,0:T(8,128)(2,1)}, f32[18,3,192,512]{3,2,1,0:T(8,128)}, f32[1,2304]{1,0:T(1,128)}, f...) custom-call(bf16[128,2304]{1,0:T(8,128)(2,1)} %acts_ref.1, bf16[256,9216]{1,0:T(8,128)(2,1)} %og_ref.1, ...), custom_call_target="tpu_custom_call" | custom-call | flops 43486543872 | bytes 42467328 | tf_op jit(solution)/shard_map/gather_stats/pallas_call | solution.py:376
  201.9 0.0 copy-start
  201.9 2.3 copy-done
  204.2 0.0 copy-start.1
  204.2 1.3 copy-done.1
  205.5 0.0 copy-start.2
  205.5 0.8 copy-done.2
  206.3 0.0 copy-start.4
  206.3 0.0 copy-start.3
  206.3 72.9 %update_weight.1 = bf16[2304,9216]{1,0:T(8,128)(2,1)} custom-call(bf16[2304,1024]{1,0:T(8,128)(2,1)S(1)} %copy-done, bf16[18,1024,512]{2,1,0:T(8,128)(2,1)} %get-tuple-element.11.og_ref, bf16[2304,9216]{1,0:T(8,128)(2,1)} %w_ref.3, f32[18,3,192,512]{3,2,1,0:T(8,128)} %get-tuple-element.12.g_ref, f32[2304,128]{1,0:T(8,128)S(1)} %copy-done.1, ...), custom_call_target="tpu_custom_call" | custom-call | flops 43486543872 | bytes 84934656 | tf_op jit(solution)/shard_map/update_weight/pallas_call | solution.py:410
  279.2 0.0 copy-done.4
  279.2 0.6 reduce
  279.8 0.0 copy-done.3
  279.8 0.6 copy.9
Async XLA Ops:
  201.9 2.3 copy-start
  204.2 1.3 copy-start.1
  205.5 0.8 copy-start.2
  206.3 73.0 %copy-start.4 = (f32[1,2304]{1,0:T(1,128)S(1)}, f32[1,2304]{1,0:T(1,128)}, u32[]{:S(2)}) copy-start(f32[1,2304]{1,0:T(1,128)} %get-tuple-element.15) | copy-start | bytes 27652
  206.3 73.6 %copy-start.3 = (f32[18,1,512]{2,1,0:T(1,128)S(1)}, f32[18,1,512]{2,1,0:T(1,128)}, u32[]{:S(2)}) copy-start(f32[18,1,512]{2,1,0:T(1,128)} %get-tuple-element.16) | copy-start | bytes 110596

commit v2 on v1

--- a/solution.py
+++ b/solution.py
@@ -15,14 +15,15 @@
 
 MESH = pl.DeviceIdType.MESH
 WIDTH = 512
-TALL = 768
-KEPT = 192
-SUB = 256
-AHEAD = 2
+BLOCKS = 1
+KEEP = 2
+DOTS = 1
+PIECES = 3
+AHEAD = 3
 LAG = 2
 SLOTS = LAG + 1
-ACTS_FORWARD = 3
-ACTS_READY = 5
+ACTS_FORWARD = 4
+ACTS_READY = 6
 
 
 def lane_sum(x):
@@ -45,7 +46,10 @@
 ):
     n, tokens, width = og_all.shape
     tile_rows = acts_t.shape[0]
-    blocks = tile_rows // TALL
+    tall = grad.shape[2]
+    kept = tall // KEEP
+    sub = tile_rows // PIECES
+    blocks = tile_rows // tall
     share = tokens // rows
     half = share // 2
     wrows = tile_rows // n
@@ -125,7 +129,7 @@
 
     def g_store(j):
         s = lax.rem(j, SLOTS)
-        return pltpu.make_async_copy(grad.at[s, :, pl.ds(TALL - KEPT, KEPT), :], g_out.at[j], g_sem.at[s])
+        return pltpu.make_async_copy(grad.at[s, :, pl.ds(tall - kept, kept), :], g_out.at[j], g_sem.at[s])
 
     acts_load = pltpu.make_async_copy(acts_ref, acts_all.at[c], misc_sem.at[0])
     acts_store = pltpu.make_async_copy(acts_t, at_out, misc_sem.at[1])
@@ -197,11 +201,11 @@
         weight = 1.0 / factor
         s = lax.rem(k, SLOTS)
         for b in range(blocks):
-            @pl.loop(0, TALL // SUB)
+            @pl.loop(0, tall // sub)
             def _(i):
-                at = pl.ds(pl.multiple_of(i * SUB, SUB), SUB)
+                at = pl.ds(pl.multiple_of(i * sub, sub), sub)
                 g = grad[s, b, at, :]
-                to = pl.ds(pl.multiple_of(b * TALL + i * SUB, SUB), SUB)
+                to = pl.ds(pl.multiple_of(b * tall + i * sub, sub), sub)
                 sacc[to, :] += lane_sum(g * g * weight)
 
     def compute(k):
@@ -218,13 +222,13 @@
         column = jnp.zeros((8, width), jnp.float32)
         for b in range(blocks):
             def step(i, column):
-                to = pl.ds(pl.multiple_of(b * TALL + i * SUB, SUB), SUB)
+                to = pl.ds(pl.multiple_of(b * tall + i * sub, sub), sub)
                 g = jnp.dot(acts_t[to, :], right[...], preferred_element_type=jnp.float32)
-                grad[s, b, pl.ds(pl.multiple_of(i * SUB, SUB), SUB), :] = g
+                grad[s, b, pl.ds(pl.multiple_of(i * sub, sub), sub), :] = g
                 squared = g * g + ADDED_SQUARE
                 rowacc[to, :] += lane_sum(squared)
                 return column + sublane_sum(squared)
-            column = lax.fori_loop(0, TALL // SUB, step, column)
+            column = lax.fori_loop(0, tall // sub, step, column)
         colx[r, k] = jnp.sum(column, axis=0, keepdims=True)
         for d in range(1, rows):
             col_copy(k, d).start()
@@ -347,17 +351,19 @@
 def update_kernel(at_ref, og_ref, w_ref, g_ref, rs_ref, cs_ref, out_ref):
     i = pl.program_id(1)
     tall, width = w_ref.shape
-    cs = cs_ref[0]
-    sub = KEPT
+    j = pl.program_id(0)
+    cs = cs_ref[j]
+    kept = tall // KEEP
+    sub = (tall - kept) // DOTS
 
     def finish(g, at):
-        rs = rs_ref[at, :]
+        rs = rs_ref[pl.ds(pl.multiple_of(i * tall + at.start, 16), at.size), :]
         wide = jnp.concatenate([rs] * (width // 128), axis=1)
         out_ref[at, :] = (w_ref[at, :].astype(jnp.float32) - g * wide * cs).astype(out_ref.dtype)
 
-    finish(g_ref[0, 0], pl.ds(tall - KEPT, KEPT))
-    for k in range((tall - KEPT) // sub):
-        left = at_ref[pl.ds(pl.multiple_of(i * tall + k * sub, sub), sub), :]
+    finish(g_ref[0, 0], pl.ds(tall - kept, kept))
+    for k in range(DOTS):
+        left = at_ref[pl.ds(pl.multiple_of(i * tall + k * sub, 16), sub), :]
         g = jnp.dot(left, og_ref[0], preferred_element_type=jnp.float32)
         finish(g, pl.ds(k * sub, sub))
 
@@ -367,18 +373,20 @@
     part = activations.shape[0]
     tokens = part * cols
     n, width = tile_cols // WIDTH, WIDTH
-    blocks = tile_rows // TALL
+    blocks = BLOCKS
+    tall = tile_rows // blocks
+    kept = tall // KEEP
     f32, bf16 = jnp.float32, jnp.bfloat16
     any_space = pl.BlockSpec(memory_space=pl.ANY)
     vmem = pl.BlockSpec(memory_space=pltpu.VMEM)
     dma = pltpu.SemaphoreType.DMA
     flops = 2 * tile_rows * tile_cols * tokens
-    og_all, acts_t, kept, new_row, new_col, rs, cs = pl.pallas_call(
+    og_all, acts_t, grads, new_row, new_col, rs, cs = pl.pallas_call(
         functools.partial(gather_kernel, rows, cols),
         out_shape=(
             jax.ShapeDtypeStruct((n, tokens, width), bf16),
             jax.ShapeDtypeStruct((tile_rows, tokens), bf16),
-            jax.ShapeDtypeStruct((n, blocks, KEPT, width), f32),
+            jax.ShapeDtypeStruct((n, blocks, kept, width), f32),
             jax.ShapeDtypeStruct((1, tile_rows), f32),
             jax.ShapeDtypeStruct((n, 1, width), f32),
             jax.ShapeDtypeStruct((tile_rows, 128), f32),
@@ -390,7 +398,7 @@
             pltpu.VMEM((n, tokens, width), bf16),
             pltpu.VMEM((cols, part, tile_rows), bf16),
             pltpu.VMEM((tile_rows, tokens), bf16),
-            pltpu.VMEM((SLOTS, blocks, TALL, width), f32),
+            pltpu.VMEM((SLOTS, blocks, tall, width), f32),
             pltpu.VMEM((2, tile_rows // n, tile_cols), bf16),
             pltpu.VMEM((tile_rows, 128), f32),
             pltpu.VMEM((tile_rows, 128), f32),
@@ -414,17 +422,17 @@
         in_specs=[
             pl.BlockSpec((tile_rows, tokens), lambda j, i: (0, 0)),
             pl.BlockSpec((1, tokens, width), lambda j, i: (j, 0, 0)),
-            pl.BlockSpec((TALL, width), lambda j, i: (i, j)),
-            pl.BlockSpec((1, 1, KEPT, width), lambda j, i: (j, i, 0, 0)),
-            pl.BlockSpec((TALL, 128), lambda j, i: (i, 0)),
-            pl.BlockSpec((1, 1, width), lambda j, i: (j, 0, 0)),
+            pl.BlockSpec((tall, width), lambda j, i: (i, j)),
+            pl.BlockSpec((1, 1, kept, width), lambda j, i: (j, i, 0, 0)),
+            vmem,
+            vmem,
         ],
-        out_specs=pl.BlockSpec((TALL, width), lambda j, i: (i, j)),
+        out_specs=pl.BlockSpec((tall, width), lambda j, i: (i, j)),
         compiler_params=pltpu.CompilerParams(
             dimension_semantics=("arbitrary", "arbitrary"), vmem_limit_bytes=48 * 1024 * 1024),
         cost_estimate=pl.CostEstimate(flops=flops, bytes_accessed=4 * weight.size, transcendentals=0),
         name="update_weight",
-    )(acts_t, og_all, weight, kept, rs, cs)
+    )(acts_t, og_all, weight, grads, rs, cs)
     return new_weight, new_row.reshape(tile_rows), new_col.reshape(tile_cols)
 
 
@@ -470,7 +478,7 @@
     chunks = tile_cols // WIDTH
     fits = (
         rows == 4 and cols % 2 == 0 and cols > 2
-        and tile_rows % TALL == 0 and tile_cols % 1024 == 0
+        and tile_rows % (64 * BLOCKS * KEEP * DOTS) == 0 and tile_rows % (16 * BLOCKS * PIECES) == 0 and tile_cols % 1024 == 0
         and chunks > ACTS_READY + SLOTS and tile_rows % (16 * chunks) == 0
         and output_grads.shape[0] % 32 == 0 and activations.shape[0] % 128 == 0
     )

time: 282 us -> 255 us (0.904)
  Pallas kernels: 273 us -> 247 us
    pallas_call x1, Pallas kernels: 200 us -> 185 us  [with_kernels(): pl.pallas_call(functools.partial(gather_kernel, rows, cols), out_shape=(j...]
    pallas_call x1, Pallas kernels: 72.9 us -> 61.6 us  [with_kernels(): pl.pallas_call(update_kernel, grid=(n, blocks), out_shape=jax.ShapeDtypeS...]
where the time goes in v2:
time: 255 us; the launch traced here: 254 us
  Pallas kernels  247 us (97%)
  local copies, waits for them, and re-layouts  6.31 us (2%)
    pallas_call x1, Pallas kernels, with_kernels(): pl.pallas_call(functools.partial(gather_kernel, rows, cols), out_shape=(j...  185 us
    pallas_call x1, Pallas kernels, with_kernels(): pl.pallas_call(update_kernel, grid=(n, blocks), out_shape=jax.ShapeDtypeS...  61.6 us

profile of v2, /device:TPU:0, one launch (start us, length us, event | category | flops | bytes accessed | tf_op | source)
XLA Modules:
  0.0 254.2 jit_solution(7034388351575643934)
XLA Ops:
  0.6 1.3 reshape.18.rm_ref
  1.9 185.0 %gather_stats.1 = (bf16[18,1024,512]{2,1,0:T(8,128)(2,1)}, bf16[2304,1024]{1,0:T(8,128)(2,1)}, f32[18,1,1152,512]{3,2,1,0:T(8,128)}, f32[1,2304]{1,0:T(1,128)}, ...) custom-call(bf16[128,2304]{1,0:T(8,128)(2,1)} %acts_ref.1, bf16[256,9216]{1,0:T(8,128)(2,1)} %og_ref.1, ...), custom_call_target="tpu_custom_call" | custom-call | flops 43486543872 | bytes 42467328 | tf_op jit(solution)/shard_map/gather_stats/pallas_call | solution.py:384
  186.9 0.0 copy-start
  187.0 2.3 copy-done
  189.3 0.0 copy-start.1
  189.3 1.3 copy-done.1
  190.6 0.0 copy-start.2
  190.6 0.8 copy-done.2
  191.3 0.0 copy-start.4
  191.3 0.0 copy-start.3
  191.3 61.6 %update_weight.1 = bf16[2304,9216]{1,0:T(8,128)(2,1)} custom-call(bf16[2304,1024]{1,0:T(8,128)(2,1)S(1)} %copy-done, bf16[18,1024,512]{2,1,0:T(8,128)(2,1)} %get-tuple-element.11.og_ref, bf16[2304,9216]{1,0:T(8,128)(2,1)} %w_ref.3, f32[18,1,1152,512]{3,2,1,0:T(8,128)} %get-tuple-element.12.g_ref, f32[2304,128]{1,0:T(8,128)S(1)} %copy-done.1, ...), custom_call_target="tpu_custom_call" | custom-call | flops 43486543872 | bytes 84934656 | tf_op jit(solution)/shard_map/update_weight/pallas_call | solution.py:418
  253.0 0.0 copy-done.4
  253.0 0.6 reduce
  253.6 0.0 copy-done.3
  253.6 0.6 copy.9
Async XLA Ops:
  186.9 2.3 copy-start
  189.3 1.3 copy-start.1
  190.6 0.8 copy-start.2
  191.3 61.6 %copy-start.4 = (f32[1,2304]{1,0:T(1,128)S(1)}, f32[1,2304]{1,0:T(1,128)}, u32[]{:S(2)}) copy-start(f32[1,2304]{1,0:T(1,128)} %get-tuple-element.15) | copy-start | bytes 27652
  191.3 62.3 %copy-start.3 = (f32[18,1,512]{2,1,0:T(1,128)S(1)}, f32[18,1,512]{2,1,0:T(1,128)}, u32[]{:S(2)}) copy-start(f32[18,1,512]{2,1,0:T(1,128)} %get-tuple-element.16) | copy-start | bytes 110596
